TPU v7x, 32 devices: a whole 2x2x4 slice. The times are simulated.
32 devices in a mesh: rep: 4 (over z), fsdp: 8 (over y, x, core).
Axes of the slice: x: 2, y: 2, z: 4, core: 2. Of those that a mesh axis runs over, the one named last changes fastest.
Arguments:
- tokens: bfloat16 [16384, 2048], P(('rep', 'fsdp')), may hold values from -6 to 6
- norm_gain: float32 [2048], replicated, may hold values from 0.5 to 1.5
- outer_params: float32 [2, 2048, 4096], P(None, 'fsdp'), may hold values from -6 to 6
- momentum: float32 [2, 2048, 4096], P(None, 'fsdp'), may hold values from -6 to 6
- deltas: bfloat16 [4, 2, 2048, 4096], P('rep', None, 'fsdp'), may hold values from -6 to 6
Outputs:
- new_params: float32 [2, 2048, 4096], P(None, 'fsdp')
- new_momentum: float32 [2, 2048, 4096], P(None, 'fsdp')
- hidden: bfloat16 [16384, 4096], P(('rep', 'fsdp'))
All inputs are finite; a program needn't handle non-finite values.
Results may differ from a plain program's by a relative error of at most 0.01.
Values may be sent and summed in bfloat16 or wider, within the bound.
A program may use at most 192 MiB of HBM per device.

v0:
```python
import math

import jax
import jax.numpy as jnp
from jax import lax
from jax.sharding import PartitionSpec as P

EPS = 1e-05
MU = 0.9
RATE = 0.7


def advance(params, moment, summed, groups):
    outer_grad = summed * (1.0 / groups)
    moment_next = MU * moment + outer_grad
    params_next = params - RATE * (outer_grad + MU * moment_next)
    return (params_next, moment_next)


def body(tokens, norm_gain, outer_params, momentum, deltas):
    groups = lax.axis_size("rep")
    own_delta = deltas[0].astype(jnp.float32)
    summed = lax.psum(own_delta.astype(jnp.bfloat16), "rep").astype(jnp.float32)
    new_params, new_momentum = advance(outer_params, momentum, summed, groups)
    weights = new_params.astype(jnp.bfloat16)
    values = tokens.astype(jnp.float32)
    scale_rows = lax.rsqrt(jnp.mean(values * values, axis=-1, keepdims=True) + EPS)
    normed = (values * scale_rows * norm_gain).astype(jnp.bfloat16)
    factor = 1.0 / math.sqrt(normed.shape[1])
    results = []
    for which in range(2):
        results.append(
            jnp.dot(
                normed,
                lax.all_gather(weights[which], "fsdp", axis=0, tiled=True),
                preferred_element_type=jnp.float32,
            )
        )
    gate, up = (results[0], results[1])
    hidden = (jax.nn.silu(gate * factor) * (up * factor)).astype(jnp.bfloat16)
    return (new_params, new_momentum, hidden)


def solution(mesh):
    in_specs = (
        P(("rep", "fsdp"), None),
        P(),
        P(None, "fsdp", None),
        P(None, "fsdp", None),
        P("rep", None, "fsdp", None),
    )
    out_specs = (P(None, "fsdp", None), P(None, "fsdp", None), P(("rep", "fsdp"), None))
    return jax.shard_map(body, mesh=mesh, in_specs=in_specs, out_specs=out_specs, check_vma=False)
```

profile of v0, /device:TPU:0, one launch (start us, length us, event | category | flops | bytes accessed | tf_op | source)
XLA Modules:
  0.0 390.7 jit_solution(17987212437413564745)
XLA Ops:
  7.2 0.0 all-reduce.2.cloned.1.call-start
  7.2 0.7 all-reduce.2.cloned.1.call-update
  7.9 0.0 all-gather.7.cloned.1.call-start
  7.9 160.1 %all-reduce.2.cloned.1.call-done = bf16[2,256,4096]{2,1,0:T(8,128)(2,1)} async-done(((bf16[2,256,4096]{2,1,0:T(8,128)(2,1)}), bf16[2,256,4096]{2,1,0:T(8,128)(2,1)}) %all-reduce.2.cloned.1.call-update) | async-done | bytes 4194320 | tf_op jit(solution)/shard_map/psum | solution.py:23
  168.1 12.3 %fusion.11 = (bf16[2,256,4096]{2,1,0:T(8,128)(2,1)S(1)}, f32[2,256,4096]{2,1,0:T(8,128)}, f32[2,256,4096]{2,1,0:T(8,128)}) fusion(f32[2,256,4096]{2,1,0:T(8,128)} %param.7, bf16[2,256,4096]{2,1,0:T(8,128)(2,1)} %all-reduce.2.cloned.1.call-done, f32[2,256,4096]{2,1,0:T(8,128)} %param.8), kind=kLoop, calls=%fused_computation.14 | loop fusion | flops 18874368 | bytes 41943040 | tf_op jit(solution)/shard_map/convert_element_type | solution.py:25
  180.3 0.0 copy-start
  180.3 0.0 copy-start.1
  180.3 2.3 fusion.12
  182.6 0.0 all-gather.7.cloned.1.call-update
  182.7 0.0 all-gather.5.cloned.1.call-start
  182.7 0.7 all-gather.5.cloned.1.call-update
  183.4 0.0 copy-done
  183.4 0.5 fusion.6
  183.9 87.6 %all-gather.7.cloned.1.call-done = bf16[1,2048,4096]{2,1,0:T(8,128)(2,1)} async-done(((bf16[1,256,4096]{2,1,0:T(8,128)(2,1)}), bf16[1,2048,4096]{2,1,0:T(8,128)(2,1)}) %all-gather.7.cloned.1.call-update) | async-done | bytes 16777232 | tf_op jit(solution)/shard_map/all_gather | solution.py:35
  271.5 0.0 copy-done.1
  271.5 14.5 %fusion = f32[512,4096]{1,0:T(8,128)} fusion(bf16[1,2048,4096]{2,1,0:T(8,128)(2,1)} %all-gather.7.cloned.1.call-done, bf16[512,2048]{1,0:T(8,128)(2,1)S(1)} %copy-done, f32[2048]{0:T(1024)S(1)} %copy-done.1, f32[512]{0:T(512)S(1)} %add_rsqrt_fusion), kind=kOutput, calls=%fused_computation | convolution fusion | flops 8594128896 | bytes 27273216 | tf_op jit(solution)/shard_map/dot_general | solution.py:33
  286.0 77.7 %all-gather.5.cloned.1.call-done = bf16[1,2048,4096]{2,1,0:T(8,128)(2,1)} async-done(((bf16[1,256,4096]{2,1,0:T(8,128)(2,1)}), bf16[1,2048,4096]{2,1,0:T(8,128)(2,1)}) %all-gather.5.cloned.1.call-update) | async-done | bytes 16777232 | tf_op jit(solution)/shard_map/all_gather | solution.py:35
  363.7 20.5 %multiply_convert_fusion = bf16[512,4096]{1,0:T(8,128)(2,1)} fusion(f32[512,4096]{1,0:T(8,128)} %fusion, bf16[1,2048,4096]{2,1,0:T(8,128)(2,1)} %all-gather.5.cloned.1.call-done, bf16[512,2048]{1,0:T(8,128)(2,1)S(1)} %copy-done, f32[2048]{0:T(1024)S(1)} %copy-done.1, f32[512]{0:T(512)S(1)} %add_rsqrt_fusion), kind=kOutput, calls=%fused_computation.4 | convolution fusion | flops 8610906112 | bytes 31467520 | tf_op jit(solution)/shard_map/dot_general | solution.py:33
  (1 shorter events, 0.0 us)
Async XLA Ops:
  7.2 160.9 %all-reduce.2.cloned.1.call-start = ((), (), s32[]{:S(2)}) async-start(), calls=%async_computation | async-start | bytes 8388608 | tf_op jit(solution)/shard_map/psum | solution.py:23
  7.9 263.6 %all-gather.7.cloned.1.call-start = ((), (), s32[]{:S(2)}) async-start(), calls=%async_computation.2 | async-start | bytes 18874368 | tf_op jit(solution)/shard_map/all_gather | solution.py:35
  180.3 3.1 copy-start
  180.3 91.2 %copy-start.1 = (f32[2048]{0:T(1024)S(1)}, f32[2048]{0:T(1024)}, u32[]{:S(2)}) copy-start(f32[2048]{0:T(1024)} %param.6) | copy-start | bytes 24580
  182.7 181.1 %all-gather.5.cloned.1.call-start = ((), (), s32[]{:S(2)}) async-start(), calls=%async_computation.1 | async-start | bytes 18874368 | tf_op jit(solution)/shard_map/all_gather | solution.py:35
Sparse Core Ops, SparseCore 0:
  10.3 157.6 all-reduce.1
  182.8 88.6 all-gather.6
  274.0 89.7 all-gather.4
where the time goes:
time: 391 us
  waiting for transfers between devices  327 us (84%)
  matrix products  35 us (9%)
  between operations  13.8 us (4%)
  other arithmetic  12.8 us (3%)
    all_gather x2, waiting for transfers between devices, body(): lax.all_gather(weights[which], 'fsdp', axis=0, tiled=True)  165 us
    psum x1, waiting for transfers between devices, body(): summed = lax.psum(own_delta.astype(jnp.bfloat16), 'rep').astype(jnp.float32)  160 us
    dot_general x2, matrix products, body(): jnp.dot(normed, lax.all_gather(weights[which], 'fsdp', axis=0, tiled=True...  35 us
    convert_element_type x1, other arithmetic, body(): weights = new_params.astype(jnp.bfloat16)  12.3 us
  transfers between devices with their start and end apart: 3, of which 3 were waited for; matrix products, arithmetic and copies ran while one was open for 4% of the time, Pallas kernels for 0%

commit v1 on v0

v1 whole, which is shorter than its diff:
```python
import functools
import math

import jax
import jax.numpy as jnp
from jax import lax
from jax.experimental import pallas as pl
from jax.experimental.pallas import tpu as pltpu
from jax.sharding import PartitionSpec as P

EPS = 1e-05
MU = 0.9
RATE = 0.7
CORES = 2
WIDTH = 256
SUM_LAG = 2
STEP_LAG = 3


def advance(params, moment, summed, groups):
    outer_grad = summed * (1.0 / groups)
    moment_next = MU * moment + outer_grad
    params_next = params - RATE * (outer_grad + MU * moment_next)
    return (params_next, moment_next)


def kernel(
    groups, shards,
    tokens, gain, params, moment, deltas,
    summed, hidden,
    full, own, part_in, peer_in, part, total, normed, p_slots, m_slots, h_slots,
    load_sem, token_sem, pm_sem, out_sem, h_sem,
    part_recv, peer_recv, total_recv, ring_recv, pair_recv,
    part_send, total_send, ring_send, pair_send,
):
    chunks, _, height, width = own.shape
    chips = shards // CORES
    half = chips // 2
    rows = normed.shape[0]
    rep = lax.axis_index("rep")
    mine = lax.axis_index("fsdp")
    core = mine % CORES
    chip = mine // CORES
    turn = half + chips - 1

    def flip(value):
        return value + (value // half) * (turn - 2 * value)

    place = flip(chip)

    def shard_at(position):
        return flip((position + chips) % chips) * CORES + core

    right, left = shard_at(place + 1), shard_at(place - 1)
    partner = chip * CORES + (1 - core)
    middle = groups // 2
    low = rep < middle
    inward = jnp.where(low, rep + 1, rep - 1)
    outward = jnp.where(low, rep - 1, rep + 1)
    at_end = (rep == 0) | (rep == groups - 1)
    at_middle = (rep == middle - 1) | (rep == middle)

    def columns(c):
        return pl.ds(pl.multiple_of(c * width, width), width)

    def block(c, which, owner):
        return full.at[c, which, pl.ds(pl.multiple_of(owner * height, height), height), :]

    def delta_load(c):
        return pltpu.make_async_copy(deltas.at[0, :, :, columns(c)], own.at[c], load_sem.at[c])

    def state_loads(c):
        slot = c % 2
        return (
            pltpu.make_async_copy(params.at[:, :, columns(c)], p_slots.at[slot], pm_sem.at[slot, 0]),
            pltpu.make_async_copy(moment.at[:, :, columns(c)], m_slots.at[slot], pm_sem.at[slot, 1]),
        )

    def part_copy(src, dst, c, recv):
        return pltpu.make_async_remote_copy(
            src_ref=src.at[c], dst_ref=dst.at[c], send_sem=part_send, recv_sem=recv.at[c],
            device_id={"rep": inward}, device_id_type=pl.DeviceIdType.MESH)

    def total_copy(c):
        return pltpu.make_async_remote_copy(
            src_ref=total.at[c], dst_ref=total.at[c], send_sem=total_send, recv_sem=total_recv.at[c],
            device_id={"rep": outward}, device_id_type=pl.DeviceIdType.MESH)

    def ring_copy(c, which, owner, hop, target):
        return pltpu.make_async_remote_copy(
            src_ref=block(c, which, owner), dst_ref=block(c, which, owner),
            send_sem=ring_send.at[which], recv_sem=ring_recv.at[c, which, hop - 1],
            device_id={"fsdp": target}, device_id_type=pl.DeviceIdType.MESH)

    def pair_copy(c, which, owner):
        return pltpu.make_async_remote_copy(
            src_ref=block(c, which, owner), dst_ref=block(c, which, owner),
            send_sem=pair_send, recv_sem=pair_recv.at[c],
            device_id={"fsdp": partner}, device_id_type=pl.DeviceIdType.MESH)

    @pl.loop(0, chunks)
    def _(c):
        delta_load(c).start()

    token_copy = pltpu.make_async_copy(tokens, normed, token_sem)
    token_copy.start()
    for copy in state_loads(0):
        copy.start()

    barrier = pltpu.get_barrier_semaphore()
    for target in (partner, left, right):
        pl.semaphore_signal(barrier, inc=1, device_id={"fsdp": target}, device_id_type=pl.DeviceIdType.MESH)
    pl.semaphore_signal(barrier, inc=1, device_id={"rep": inward}, device_id_type=pl.DeviceIdType.MESH)

    @pl.when(jnp.logical_not(at_end))
    def _():
        pl.semaphore_signal(barrier, inc=1, device_id={"rep": outward}, device_id_type=pl.DeviceIdType.MESH)
        pl.semaphore_wait(barrier, 5)

    @pl.when(at_end)
    def _():
        pl.semaphore_wait(barrier, 4)

    @pl.loop(0, chunks)
    def _(c):
        delta_load(c).wait()

        @pl.when(at_end & jnp.logical_not(at_middle))
        def _():
            part_copy(own, part_in, c, part_recv).start()

        @pl.when(at_end & at_middle)
        def _():
            part_copy(own, peer_in, c, peer_recv).start()

    token_copy.wait()
    piece = 64

    @pl.loop(0, rows // piece)
    def _(i):
        at = pl.ds(pl.multiple_of(i * piece, piece), piece)
        values = normed[at, :].astype(jnp.float32)
        scale = lax.rsqrt(jnp.mean(values * values, axis=-1, keepdims=True) + EPS)
        normed[at, :] = (values * scale * gain[...]).astype(jnp.bfloat16)

    factor = 1.0 / math.sqrt(normed.shape[1])
    last = chips - 1

    def live(c):
        return (c >= 0) & (c < chunks)

    @pl.loop(0, chunks + STEP_LAG + chips)
    def _(t):
        for hop in range(last, 0, -1):
            c = t - STEP_LAG - hop

            @pl.when(live(c))
            def _(c=c, hop=hop):
                for which, owner, target in ((0, shard_at(place - hop), right), (1, shard_at(place + hop), left)):
                    ring_copy(c, which, owner, hop, target).wait_recv()
                    if hop < last:
                        ring_copy(c, which, owner, hop + 1, target).start()
                    pair_copy(c, which, owner).start()

        u = t - STEP_LAG

        @pl.when(live(u))
        def _():
            @pl.when(jnp.logical_not(at_middle))
            def _():
                total_copy(u).wait_recv()

                @pl.when(jnp.logical_not(at_end))
                def _():
                    total_copy(u).start()

            @pl.when(u + 1 < chunks)
            def _():
                for copy in state_loads(u + 1):
                    copy.start()

            for copy in state_loads(u):
                copy.wait()
            slot = u % 2
            at = pl.ds(pl.multiple_of(mine * height, height), height)
            for which, target in ((0, right), (1, left)):
                stepped, _ = advance(
                    p_slots[slot, which], m_slots[slot, which], total[u, which].astype(jnp.float32), groups)
                full[u, which, at, :] = stepped.astype(jnp.bfloat16)
                ring_copy(u, which, mine, 1, target).start()
                pair_copy(u, which, mine).start()
            pltpu.make_async_copy(total.at[u], summed.at[:, :, columns(u)], out_sem).start()

        s = t - SUM_LAG

        @pl.when(live(s) & at_middle)
        def _():
            part_copy(part, peer_in, s, peer_recv).wait_recv()

            @pl.when(at_end)
            def _():
                total[s] = (own[s].astype(jnp.float32) + peer_in[s].astype(jnp.float32)).astype(jnp.bfloat16)

            @pl.when(jnp.logical_not(at_end))
            def _():
                total[s] = (part[s].astype(jnp.float32) + peer_in[s].astype(jnp.float32)).astype(jnp.bfloat16)
                total_copy(s).start()

        @pl.when((t < chunks) & jnp.logical_not(at_end))
        def _():
            part_copy(part, part_in, t, part_recv).wait_recv()
            part[t] = (own[t].astype(jnp.float32) + part_in[t].astype(jnp.float32)).astype(jnp.bfloat16)

            @pl.when(at_middle)
            def _():
                part_copy(part, peer_in, t, peer_recv).start()

            @pl.when(jnp.logical_not(at_middle))
            def _():
                part_copy(part, part_in, t, part_recv).start()

        c = t - STEP_LAG - chips

        @pl.when(live(c))
        def _():
            arrived = full.at[c, :, 0:chips * height, :]
            pltpu.make_async_copy(arrived, arrived, pair_recv.at[c]).wait()
            slot = c % 2

            @pl.when(c >= 2)
            def _():
                pltpu.make_async_copy(h_slots.at[slot], hidden.at[:, columns(c)], h_sem.at[slot]).wait()

            tall = rows // 2

            @pl.loop(0, 2)
            def _(i):
                at = pl.ds(pl.multiple_of(i * tall, tall), tall)
                gate = jnp.dot(normed[at, :], full[c, 0], preferred_element_type=jnp.float32) * factor
                up = jnp.dot(normed[at, :], full[c, 1], preferred_element_type=jnp.float32) * factor
                h_slots[slot, at, :] = (gate / (1.0 + jnp.exp(-gate)) * up).astype(jnp.bfloat16)

            pltpu.make_async_copy(h_slots.at[slot], hidden.at[:, columns(c)], h_sem.at[slot]).start()

    for slot in range(2):
        pltpu.make_async_copy(h_slots.at[slot], hidden.at[:, columns(0)], h_sem.at[slot]).wait()
    pltpu.make_async_copy(own, own, part_send).wait()
    pltpu.make_async_copy(total, total, out_sem).wait()

    @pl.when(jnp.logical_not(at_end))
    def _():
        pltpu.make_async_copy(total, total, total_send).wait()

    for which in range(2):
        sent = full.at[:, which, 0:last * height, :]
        pltpu.make_async_copy(sent, sent, ring_send.at[which]).wait()
    sent = full.at[:, :, 0:chips * height, :]
    pltpu.make_async_copy(sent, sent, pair_send).wait()


def solution(mesh):
    groups, shards = mesh.shape["rep"], mesh.shape["fsdp"]
    chips = shards // CORES

    def body(tokens, norm_gain, outer_params, momentum, deltas):
        rows, model = tokens.shape
        _, height, hid = outer_params.shape
        width = WIDTH
        chunks = hid // width
        bf16, f32 = jnp.bfloat16, jnp.float32
        dma = pltpu.SemaphoreType.DMA
        strip = pltpu.VMEM((chunks, 2, height, width), bf16)
        anywhere = pl.BlockSpec(memory_space=pl.ANY)
        summed, hidden = pl.pallas_call(
            functools.partial(kernel, groups, shards),
            out_shape=(
                jax.ShapeDtypeStruct(outer_params.shape, bf16),
                jax.ShapeDtypeStruct((rows, hid), bf16),
            ),
            in_specs=[anywhere, pl.BlockSpec(memory_space=pltpu.VMEM), anywhere, anywhere, anywhere],
            out_specs=(anywhere, anywhere),
            scratch_shapes=[
                pltpu.VMEM((chunks, 2, model, width), bf16),
                strip, strip, strip, strip, strip,
                pltpu.VMEM((rows, model), bf16),
                pltpu.VMEM((2, 2, height, width), f32),
                pltpu.VMEM((2, 2, height, width), f32),
                pltpu.VMEM((2, rows, width), bf16),
                dma((chunks,)), dma, dma((2, 2)), dma, dma((2,)),
                dma((chunks,)), dma((chunks,)), dma((chunks,)), dma((chunks, 2, chips - 1)), dma((chunks,)),
                dma, dma, dma((2,)), dma,
            ],
            compiler_params=pltpu.CompilerParams(
                collective_id=0, has_side_effects=True, vmem_limit_bytes=62 * 1024 * 1024),
            name="round",
        )(tokens, norm_gain.reshape(1, model), outer_params, momentum, deltas)
        new_params, new_momentum = advance(outer_params, momentum, summed.astype(f32), groups)
        return (new_params, new_momentum, hidden)

    in_specs = (
        P(("rep", "fsdp"), None),
        P(),
        P(None, "fsdp", None),
        P(None, "fsdp", None),
        P("rep", None, "fsdp", None),
    )
    out_specs = (P(None, "fsdp", None), P(None, "fsdp", None), P(("rep", "fsdp"), None))
    return jax.shard_map(body, mesh=mesh, in_specs=in_specs, out_specs=out_specs, check_vma=False)
```

time: 391 us -> 185 us (0.47)
  waiting for transfers between devices: 327 us -> 0 us
  Pallas kernels: 0 us -> 170 us
  matrix products: 35 us -> 0 us
  between operations: 13.8 us -> 0.65 us
    pallas_call x0 -> x1, Pallas kernels: none -> 170 us  [body(): pl.pallas_call(functools.partial(kernel, groups, shards), out_shape=(jax....]
    all_gather x2 -> x0, waiting for transfers between devices: 165 us -> none  [body(): lax.all_gather(weights[which], 'fsdp', axis=0, tiled=True)]
    psum x1 -> x0, waiting for transfers between devices: 160 us -> none  [body(): summed = lax.psum(own_delta.astype(jnp.bfloat16), 'rep').astype(jnp.float32)]
    dot_general x2 -> x0, matrix products: 35 us -> none  [body(): jnp.dot(normed, lax.all_gather(weights[which], 'fsdp', axis=0, tiled=True...]
    sub x0 -> x1, other arithmetic: none -> 12.7 us  [advance(): params_next = params - RATE * (outer_grad + MU * moment_next)]
    convert_element_type x1 -> x0, other arithmetic: 12.3 us -> none  [body(): weights = new_params.astype(jnp.bfloat16)]
  transfers between devices with their start and end apart: 3 -> 0, of which waited for: 3 -> 0; matrix products, arithmetic and copies ran while one was open for 4% -> 0% of each run, Pallas kernels for 0% -> 0%
where the time goes in v1:
time: 185 us
  Pallas kernels  170 us (92%)
  other arithmetic  12.7 us (7%)
  local copies, waits for them, and re-layouts  2.02 us (1%)
    pallas_call x1, Pallas kernels, body(): pl.pallas_call(functools.partial(kernel, groups, shards), out_shape=(jax....  170 us
    sub x1, other arithmetic, advance(): params_next = params - RATE * (outer_grad + MU * moment_next)  12.7 us

profile of v1, /device:TPU:0, one launch (start us, length us, event | category | flops | bytes accessed | tf_op | source)
XLA Modules:
  0.0 185.0 jit_solution(7278880389562823278)
XLA Ops:
  0.6 169.6 %round.1 = (bf16[2,256,4096]{2,1,0:T(8,128)(2,1)}, bf16[512,4096]{1,0:T(8,128)(2,1)}) custom-call(bf16[512,2048]{1,0:T(8,128)(2,1)} %tokens.1, f32[1,2048]{1,0:T(1,128)} %bitcast.1, f32[2,256,4096]{2,1,0:T(8,128)} %params.1, f32[2,256,4096]{2,1,0:T(8,128)} %moment.1, bf16[1,2,256,4096]{3,2,1,0:T(8,128)(2,1)} %deltas.1), custom_call_target="tpu_custom_call" | custom-call | tf_op jit(solution)/shard_map/round/pallas_call | solution.py:274
  170.3 0.0 copy-start
  170.3 12.7 %multiply_subtract_fusion = (f32[2,256,4096]{2,1,0:T(8,128)}, f32[2,256,4096]{2,1,0:T(8,128)}) fusion(f32[2,256,4096]{2,1,0:T(8,128)} %params.1, bf16[2,256,4096]{2,1,0:T(8,128)(2,1)} %get-tuple-element.5, f32[2,256,4096]{2,1,0:T(8,128)} %moment.1), kind=kLoop, calls=%fused_computation | loop fusion | flops 16777216 | bytes 37748736 | tf_op jit(solution)/shard_map/sub | solution.py:23
  183.0 0.0 copy-done
  183.0 2.0 %copy.9 = bf16[512,4096]{1,0:T(8,128)(2,1)} copy(bf16[512,4096]{1,0:T(8,128)(2,1)S(1)} %copy-done) | data formatting | bytes 8388608
Async XLA Ops:
  170.3 12.7 %copy-start = (bf16[512,4096]{1,0:T(8,128)(2,1)S(1)}, bf16[512,4096]{1,0:T(8,128)(2,1)}, u32[]{:S(2)}) copy-start(bf16[512,4096]{1,0:T(8,128)(2,1)} %get-tuple-element.14) | copy-start | bytes 12582916

commit v2 on v1

--- a/solution.py
+++ b/solution.py
@@ -13,8 +13,9 @@
 RATE = 0.7
 CORES = 2
 WIDTH = 256
-SUM_LAG = 2
-STEP_LAG = 3
+SUM_LAG = 1
+STEP_LAG = 2
+SPLIT = 2
 
 
 def advance(params, moment, summed, groups):
@@ -27,13 +28,15 @@
 def kernel(
     groups, shards,
     tokens, gain, params, moment, deltas,
-    summed, hidden,
-    full, own, part_in, peer_in, part, total, normed, p_slots, m_slots, h_slots,
-    load_sem, token_sem, pm_sem, out_sem, h_sem,
+    p_out, m_out, hidden,
+    full, own, peer_in, total, normed, h_slots,
+    load_sem, token_sem, pm_sem, h_sem,
     part_recv, peer_recv, total_recv, ring_recv, pair_recv,
     part_send, total_send, ring_send, pair_send,
 ):
-    chunks, _, height, width = own.shape
+    chunks, pieces, low_height, width = own.shape
+    split = pieces // 2
+    height = low_height * split
     chips = shards // CORES
     half = chips // 2
     rows = normed.shape[0]
@@ -66,24 +69,24 @@
     def block(c, which, owner):
         return full.at[c, which, pl.ds(pl.multiple_of(owner * height, height), height), :]
 
-    def delta_load(c):
-        return pltpu.make_async_copy(deltas.at[0, :, :, columns(c)], own.at[c], load_sem.at[c])
+    def delta_load(c, q):
+        at = pl.ds((q % split) * low_height, low_height)
+        return pltpu.make_async_copy(deltas.at[0, q // split, at, columns(c)], own.at[c, q], load_sem.at[c])
 
     def state_loads(c):
-        slot = c % 2
         return (
-            pltpu.make_async_copy(params.at[:, :, columns(c)], p_slots.at[slot], pm_sem.at[slot, 0]),
-            pltpu.make_async_copy(moment.at[:, :, columns(c)], m_slots.at[slot], pm_sem.at[slot, 1]),
+            pltpu.make_async_copy(params.at[:, :, columns(c)], p_out.at[:, :, columns(c)], pm_sem.at[c % 2, 0]),
+            pltpu.make_async_copy(moment.at[:, :, columns(c)], m_out.at[:, :, columns(c)], pm_sem.at[c % 2, 1]),
         )
 
-    def part_copy(src, dst, c, recv):
+    def part_copy(dst, c, q, recv):
         return pltpu.make_async_remote_copy(
-            src_ref=src.at[c], dst_ref=dst.at[c], send_sem=part_send, recv_sem=recv.at[c],
+            src_ref=own.at[c, q], dst_ref=dst.at[c, q], send_sem=part_send, recv_sem=recv.at[c, q],
             device_id={"rep": inward}, device_id_type=pl.DeviceIdType.MESH)
 
-    def total_copy(c):
+    def total_copy(c, q):
         return pltpu.make_async_remote_copy(
-            src_ref=total.at[c], dst_ref=total.at[c], send_sem=total_send, recv_sem=total_recv.at[c],
+            src_ref=total.at[c, q], dst_ref=total.at[c, q], send_sem=total_send, recv_sem=total_recv.at[c, q],
             device_id={"rep": outward}, device_id_type=pl.DeviceIdType.MESH)
 
     def ring_copy(c, which, owner, hop, target):
@@ -100,7 +103,8 @@
 
     @pl.loop(0, chunks)
     def _(c):
-        delta_load(c).start()
+        for q in range(pieces):
+            delta_load(c, q).start()
 
     token_copy = pltpu.make_async_copy(tokens, normed, token_sem)
     token_copy.start()
@@ -123,15 +127,17 @@
 
     @pl.loop(0, chunks)
     def _(c):
-        delta_load(c).wait()
+        pltpu.make_async_copy(own.at[c], own.at[c], load_sem.at[c]).wait()
 
         @pl.when(at_end & jnp.logical_not(at_middle))
         def _():
-            part_copy(own, part_in, c, part_recv).start()
+            for q in range(pieces):
+                part_copy(total, c, q, part_recv).start()
 
         @pl.when(at_end & at_middle)
         def _():
-            part_copy(own, peer_in, c, peer_recv).start()
+            for q in range(pieces):
+                part_copy(peer_in, c, q, peer_recv).start()
 
     token_copy.wait()
     piece = 64
@@ -166,14 +172,6 @@
 
         @pl.when(live(u))
         def _():
-            @pl.when(jnp.logical_not(at_middle))
-            def _():
-                total_copy(u).wait_recv()
-
-                @pl.when(jnp.logical_not(at_end))
-                def _():
-                    total_copy(u).start()
-
             @pl.when(u + 1 < chunks)
             def _():
                 for copy in state_loads(u + 1):
@@ -181,43 +179,54 @@
 
             for copy in state_loads(u):
                 copy.wait()
-            slot = u % 2
-            at = pl.ds(pl.multiple_of(mine * height, height), height)
             for which, target in ((0, right), (1, left)):
-                stepped, _ = advance(
-                    p_slots[slot, which], m_slots[slot, which], total[u, which].astype(jnp.float32), groups)
-                full[u, which, at, :] = stepped.astype(jnp.bfloat16)
+                @pl.when(jnp.logical_not(at_middle))
+                def _(which=which):
+                    for q in range(which * split, (which + 1) * split):
+                        total_copy(u, q).wait_recv()
+
+                        @pl.when(jnp.logical_not(at_end))
+                        def _(q=q):
+                            total_copy(u, q).start()
+
+                for q in range(which * split, (which + 1) * split):
+                    rows_here = slice((q % split) * low_height, (q % split + 1) * low_height)
+                    stepped, moved = advance(
+                        p_out[which, rows_here, columns(u)], m_out[which, rows_here, columns(u)],
+                        total[u, q].astype(jnp.float32), groups)
+                    p_out[which, rows_here, columns(u)] = stepped
+                    m_out[which, rows_here, columns(u)] = moved
+                    start = mine * height + (q % split) * low_height
+                    at = pl.ds(pl.multiple_of(start, low_height), low_height)
+                    full[u, which, at, :] = stepped.astype(jnp.bfloat16)
                 ring_copy(u, which, mine, 1, target).start()
                 pair_copy(u, which, mine).start()
-            pltpu.make_async_copy(total.at[u], summed.at[:, :, columns(u)], out_sem).start()
 
         s = t - SUM_LAG
 
         @pl.when(live(s) & at_middle)
         def _():
-            part_copy(part, peer_in, s, peer_recv).wait_recv()
-
-            @pl.when(at_end)
-            def _():
-                total[s] = (own[s].astype(jnp.float32) + peer_in[s].astype(jnp.float32)).astype(jnp.bfloat16)
-
-            @pl.when(jnp.logical_not(at_end))
-            def _():
-                total[s] = (part[s].astype(jnp.float32) + peer_in[s].astype(jnp.float32)).astype(jnp.bfloat16)
-                total_copy(s).start()
+            for q in range(pieces):
+                part_copy(peer_in, s, q, peer_recv).wait_recv()
+                total[s, q] = (own[s, q].astype(jnp.float32) + peer_in[s, q].astype(jnp.float32)).astype(jnp.bfloat16)
+
+                @pl.when(jnp.logical_not(at_end))
+                def _(q=q):
+                    total_copy(s, q).start()
 
         @pl.when((t < chunks) & jnp.logical_not(at_end))
         def _():
-            part_copy(part, part_in, t, part_recv).wait_recv()
-            part[t] = (own[t].astype(jnp.float32) + part_in[t].astype(jnp.float32)).astype(jnp.bfloat16)
-
-            @pl.when(at_middle)
-            def _():
-                part_copy(part, peer_in, t, peer_recv).start()
-
-            @pl.when(jnp.logical_not(at_middle))
-            def _():
-                part_copy(part, part_in, t, part_recv).start()
+            for q in range(pieces):
+                part_copy(total, t, q, part_recv).wait_recv()
+                own[t, q] = (own[t, q].astype(jnp.float32) + total[t, q].astype(jnp.float32)).astype(jnp.bfloat16)
+
+                @pl.when(at_middle)
+                def _(q=q):
+                    part_copy(peer_in, t, q, peer_recv).start()
+
+                @pl.when(jnp.logical_not(at_middle))
+                def _(q=q):
+                    part_copy(total, t, q, part_recv).start()
 
         c = t - STEP_LAG - chips
 
@@ -245,7 +254,6 @@
     for slot in range(2):
         pltpu.make_async_copy(h_slots.at[slot], hidden.at[:, columns(0)], h_sem.at[slot]).wait()
     pltpu.make_async_copy(own, own, part_send).wait()
-    pltpu.make_async_copy(total, total, out_sem).wait()
 
     @pl.when(jnp.logical_not(at_end))
     def _():
@@ -269,32 +277,31 @@
         chunks = hid // width
         bf16, f32 = jnp.bfloat16, jnp.float32
         dma = pltpu.SemaphoreType.DMA
-        strip = pltpu.VMEM((chunks, 2, height, width), bf16)
+        strip = pltpu.VMEM((chunks, 2 * SPLIT, height // SPLIT, width), bf16)
+        each = dma((chunks, 2 * SPLIT))
         anywhere = pl.BlockSpec(memory_space=pl.ANY)
-        summed, hidden = pl.pallas_call(
+        new_params, new_momentum, hidden = pl.pallas_call(
             functools.partial(kernel, groups, shards),
             out_shape=(
-                jax.ShapeDtypeStruct(outer_params.shape, bf16),
+                pltpu.VMEM(outer_params.shape, f32),
+                pltpu.VMEM(outer_params.shape, f32),
                 jax.ShapeDtypeStruct((rows, hid), bf16),
             ),
             in_specs=[anywhere, pl.BlockSpec(memory_space=pltpu.VMEM), anywhere, anywhere, anywhere],
-            out_specs=(anywhere, anywhere),
+            out_specs=(pl.BlockSpec(memory_space=pltpu.VMEM), pl.BlockSpec(memory_space=pltpu.VMEM), anywhere),
             scratch_shapes=[
                 pltpu.VMEM((chunks, 2, model, width), bf16),
-                strip, strip, strip, strip, strip,
+                strip, strip, strip,
                 pltpu.VMEM((rows, model), bf16),
-                pltpu.VMEM((2, 2, height, width), f32),
-                pltpu.VMEM((2, 2, height, width), f32),
                 pltpu.VMEM((2, rows, width), bf16),
-                dma((chunks,)), dma, dma((2, 2)), dma, dma((2,)),
-                dma((chunks,)), dma((chunks,)), dma((chunks,)), dma((chunks, 2, chips - 1)), dma((chunks,)),
+                dma((chunks,)), dma, dma((2, 2)), dma((2,)),
+                each, each, each, dma((chunks, 2, chips - 1)), dma((chunks,)),
                 dma, dma, dma((2,)), dma,
             ],
             compiler_params=pltpu.CompilerParams(
-                collective_id=0, has_side_effects=True, vmem_limit_bytes=62 * 1024 * 1024),
+                collective_id=0, has_side_effects=True, vmem_limit_bytes=191 * 256 * 1024),
             name="round",
         )(tokens, norm_gain.reshape(1, model), outer_params, momentum, deltas)
-        new_params, new_momentum = advance(outer_params, momentum, summed.astype(f32), groups)
         return (new_params, new_momentum, hidden)
 
     in_specs = (

time: 185 us -> 179 us (0.968)
  other arithmetic: 12.7 us -> 0 us
  local copies, waits for them, and re-layouts: 2.02 us -> 10.6 us
  Pallas kernels: 170 us -> 167 us
    sub x1 -> x0, other arithmetic: 12.7 us -> none  [advance(): params_next = params - RATE * (outer_grad + MU * moment_next)]
    unnamed x3 -> x5, local copies, waits for them, and re-layouts: 2.02 us -> 10.6 us
    pallas_call x1, Pallas kernels: 170 us -> 167 us  [body(): pl.pallas_call(functools.partial(kernel, groups, shards), out_shape=(pltp...]
where the time goes in v2:
time: 179 us; the launch traced here: 178 us
  Pallas kernels  167 us (93%)
  local copies, waits for them, and re-layouts  10.6 us (6%)
    pallas_call x1, Pallas kernels, body(): pl.pallas_call(functools.partial(kernel, groups, shards), out_shape=(pltp...  167 us
    unnamed x5, local copies, waits for them, and re-layouts  10.6 us

profile of v2, /device:TPU:0, one launch (start us, length us, event | category | flops | bytes accessed | tf_op | source)
XLA Modules:
  0.0 178.4 jit_solution(2165185484887914633)
XLA Ops:
  0.6 167.1 %round.1 = (f32[2,256,4096]{2,1,0:T(8,128)S(1)}, f32[2,256,4096]{2,1,0:T(8,128)S(1)}, bf16[512,4096]{1,0:T(8,128)(2,1)}) custom-call(bf16[512,2048]{1,0:T(8,128)(2,1)} %tokens.1, f32[1,2048]{1,0:T(1,128)} %bitcast.1, f32[2,256,4096]{2,1,0:T(8,128)} %params.1, f32[2,256,4096]{2,1,0:T(8,128)} %moment.1, bf16[1,2,256,4096]{3,2,1,0:T(8,128)(2,1)} %deltas.1), custom_call_target="tpu_custom_call" | custom-call | tf_op jit(solution)/shard_map/round/pallas_call | solution.py:283
  167.8 3.4 %copy.11 = f32[2,256,4096]{2,1,0:T(8,128)} copy(f32[2,256,4096]{2,1,0:T(8,128)S(1)} %get-tuple-element.3) | data formatting | bytes 16777216
  171.2 0.0 copy-start
  171.2 4.3 %copy.12 = f32[2,256,4096]{2,1,0:T(8,128)} copy(f32[2,256,4096]{2,1,0:T(8,128)S(1)} %get-tuple-element.4) | data formatting | bytes 16777216
  175.4 1.0 copy-done
  176.4 2.0 %copy.13 = bf16[512,4096]{1,0:T(8,128)(2,1)} copy(bf16[512,4096]{1,0:T(8,128)(2,1)S(1)} %copy-done) | data formatting | bytes 8388608
Async XLA Ops:
  171.2 5.2 %copy-start = (bf16[512,4096]{1,0:T(8,128)(2,1)S(1)}, bf16[512,4096]{1,0:T(8,128)(2,1)}, u32[]{:S(2)}) copy-start(bf16[512,4096]{1,0:T(8,128)(2,1)} %get-tuple-element.11) | copy-start | bytes 12582916
